TPU v7x, 32 devices: a whole 2x2x4 slice. The times are simulated.
32 devices in a mesh: gy: 8 (over y, x, core), gx: 4 (over z).
Axes of the slice: x: 2, y: 2, z: 4, core: 2. Of those that a mesh axis runs over, the one named last changes fastest.
Arguments:
- left_factor: bfloat16 [8192, 2048], P('gy', 'gx'), may hold values from -6 to 6
- right_factor: bfloat16 [2048, 8192], P('gy', 'gx'), may hold values from -0.125 to 0.125
Outputs:
- corrected: float32 [8192, 8192], P('gy', 'gx')
All inputs are finite; a program needn't handle non-finite values.
Results may differ from a plain program's by a relative error of at most 0.0003.
Values may be sent and summed in bfloat16 or wider, within the bound.
A program may use at most 192 MiB of HBM per device.

v0:
```python
import jax
import jax.numpy as jnp
from jax import lax
from jax.sharding import PartitionSpec as P


def absorb_panel(left_panel, right_panel):
    return jnp.dot(left_panel, right_panel, preferred_element_type=jnp.float32)


def per_device(left_factor, right_factor):
    right_line = lax.all_gather(right_factor, "gy", axis=0, tiled=True)
    total = absorb_panel(lax.all_gather(left_factor, "gx", axis=1, tiled=True), right_line)
    corrected = total
    row_power = lax.psum(jnp.sum(corrected * corrected, axis=1), "gx")
    corrected = (
        corrected
        * lax.rsqrt(row_power / (corrected.shape[1] * lax.axis_size("gx")) + 1e-06)[:, None]
    )
    return corrected


def solution(mesh):
    placed = (P("gy", "gx"), P("gy", "gx"))
    return jax.shard_map(
        per_device, mesh=mesh, in_specs=placed, out_specs=P("gy", "gx"), check_vma=False
    )
```

profile of v0, /device:TPU:0, one launch (start us, length us, event | category | flops | bytes accessed | tf_op | source)
XLA Modules:
  0.0 187.5 jit_solution(11503262630804149918)
XLA Ops:
  6.5 0.0 all-gather.3.cloned.1.call-start
  6.5 0.7 all-gather.3.cloned.1.call-update
  7.3 0.0 all-gather.5.cloned.1.call-start
  7.3 0.7 all-gather.5.cloned.1.call-update
  8.0 84.4 %all-gather.3.cloned.1.call-done = bf16[1024,2048]{1,0:T(8,128)(2,1)} async-done(((bf16[1024,512]{1,0:T(8,128)(2,1)}), bf16[1024,2048]{1,0:T(8,128)(2,1)}) %all-gather.3.cloned.1.call-update) | async-done | bytes 4194320 | tf_op jit(solution)/shard_map/all_gather | solution.py:13
  92.4 54.7 %all-gather.5.cloned.1.call-done = bf16[2048,2048]{1,0:T(8,128)(2,1)} async-done(((bf16[256,2048]{1,0:T(8,128)(2,1)}), bf16[2048,2048]{1,0:T(8,128)(2,1)}) %all-gather.5.cloned.1.call-update) | async-done | bytes 8388624 | tf_op jit(solution)/shard_map/all_gather | solution.py:12
  147.1 14.5 %multiply_reduce_fusion = (f32[1024]{0:T(1024)S(1)}, f32[1024,2048]{1,0:T(8,128)}) fusion(bf16[1024,2048]{1,0:T(8,128)(2,1)} %all-gather.3.cloned.1.call-done, bf16[2048,2048]{1,0:T(8,128)(2,1)} %all-gather.5.cloned.1.call-done), kind=kOutput, calls=%fused_computation | convolution fusion | flops 8594127872 | bytes 20975616 | tf_op jit(solution)/shard_map/dot_general | solution.py:8
  161.6 11.7 %psum.7 = f32[1024]{0:T(1024)S(1)} all-reduce(f32[1024]{0:T(1024)S(1)} %get-tuple-element.5), channel_id=1, replica_groups=mesh['gy'=8,'gx'=4] {'gx'}, use_global_device_ids=true, to_apply=%region_1.0 | all-reduce | flops 1024 | bytes 8192 | tf_op jit(solution)/shard_map/psum | solution.py:15
  173.3 7.4 %broadcast_multiply_fusion = f32[1024,2048]{1,0:T(8,128)} fusion(f32[1024,2048]{1,0:T(8,128)} %get-tuple-element.6, f32[1024]{0:T(1024)S(1)} %add_rsqrt_fusion), kind=kLoop, calls=%fused_computation.1 | loop fusion | flops 2097152 | bytes 16781312 | tf_op jit(solution)/shard_map/mul | solution.py:17
  (1 shorter events, 0.0 us)
Async XLA Ops:
  6.5 85.9 %all-gather.3.cloned.1.call-start = ((), (), s32[]{:S(2)}) async-start(), calls=%async_computation | async-start | bytes 5242880 | tf_op jit(solution)/shard_map/all_gather | solution.py:13
  7.3 139.8 %all-gather.5.cloned.1.call-start = ((), (), s32[]{:S(2)}) async-start(), calls=%async_computation.1 | async-start | bytes 9437184 | tf_op jit(solution)/shard_map/all_gather | solution.py:12
Sparse Core Ops, SparseCore 0:
  8.9 83.4 all-gather.2
  94.3 52.7 all-gather.4
where the time goes:
time: 188 us
  waiting for transfers between devices  140 us (74%)
  matrix products  14.5 us (8%)
  between operations  13.4 us (7%)
  blocking collectives  11.7 us (6%)
  other arithmetic  7.4 us (4%)
    all_gather x1, waiting for transfers between devices, per_device(): lax.all_gather(left_factor, 'gx', axis=1, tiled=True)  84.4 us
    all_gather x1, waiting for transfers between devices, per_device(): right_line = lax.all_gather(right_factor, 'gy', axis=0, tiled=True)  54.7 us
    dot_general x1, matrix products, absorb_panel(): return jnp.dot(left_panel, right_panel, preferred_element_type=jnp.float32)  14.5 us
    psum x1, blocking collectives, per_device(): row_power = lax.psum(jnp.sum(corrected * corrected, axis=1), 'gx')  11.7 us
    mul x1, other arithmetic, per_device(): corrected * lax.rsqrt(row_power / (corrected.shape[1] * lax.axis_size('gx...  7.39 us
  transfers between devices with their start and end apart: 2, of which 2 were waited for; matrix products, arithmetic and copies ran while one was open for 0% of the time, Pallas kernels for 0%

commit v1 on v0

--- a/solution.py
+++ b/solution.py
@@ -12,7 +12,9 @@
     right_line = lax.all_gather(right_factor, "gy", axis=0, tiled=True)
     total = absorb_panel(lax.all_gather(left_factor, "gx", axis=1, tiled=True), right_line)
     corrected = total
-    row_power = lax.psum(jnp.sum(corrected * corrected, axis=1), "gx")
+    block = jnp.sum(corrected * corrected, axis=1)
+    parts = lax.all_gather(block, "gx", axis=0, tiled=False)
+    row_power = parts.sum(axis=0)
     corrected = (
         corrected
         * lax.rsqrt(row_power / (corrected.shape[1] * lax.axis_size("gx")) + 1e-06)[:, None]

time: 188 us -> 189 us (level)
    all_gather x0 -> x1, blocking collectives: none -> 13.2 us  [per_device(): parts = lax.all_gather(block, 'gx', axis=0, tiled=False)]
    psum x1 -> x0, blocking collectives: 11.7 us -> none  [per_device(): row_power = lax.psum(jnp.sum(corrected * corrected, axis=1), 'gx')]
where the time goes in v1:
time: 189 us
  waiting for transfers between devices  140 us (74%)
  matrix products  14.5 us (8%)
  between operations  13.4 us (7%)
  blocking collectives  13.2 us (7%)
  other arithmetic  7.41 us (4%)
    all_gather x1, waiting for transfers between devices, per_device(): lax.all_gather(left_factor, 'gx', axis=1, tiled=True)  84.4 us
    all_gather x1, waiting for transfers between devices, per_device(): right_line = lax.all_gather(right_factor, 'gy', axis=0, tiled=True)  54.7 us
    dot_general x1, matrix products, absorb_panel(): return jnp.dot(left_panel, right_panel, preferred_element_type=jnp.float32)  14.5 us
    all_gather x1, blocking collectives, per_device(): parts = lax.all_gather(block, 'gx', axis=0, tiled=False)  13.2 us
    mul x1, other arithmetic, per_device(): corrected * lax.rsqrt(row_power / (corrected.shape[1] * lax.axis_size('gx...  7.39 us
  transfers between devices with their start and end apart: 2, of which 2 were waited for; matrix products, arithmetic and copies ran while one was open for 0% of the time, Pallas kernels for 0%

profile of v1, /device:TPU:0, one launch (start us, length us, event | category | flops | bytes accessed | tf_op | source)
XLA Modules:
  0.0 189.1 jit_solution(4096460527689829625)
XLA Ops:
  6.5 0.0 all-gather.4.cloned.1.call-start
  6.5 0.7 all-gather.4.cloned.1.call-update
  7.3 0.0 all-gather.6.cloned.1.call-start
  7.3 0.7 all-gather.6.cloned.1.call-update
  8.0 84.4 %all-gather.4.cloned.1.call-done = bf16[1024,2048]{1,0:T(8,128)(2,1)} async-done(((bf16[1024,512]{1,0:T(8,128)(2,1)}), bf16[1024,2048]{1,0:T(8,128)(2,1)}) %all-gather.4.cloned.1.call-update) | async-done | bytes 4194320 | tf_op jit(solution)/shard_map/all_gather | solution.py:13
  92.4 54.7 %all-gather.6.cloned.1.call-done = bf16[2048,2048]{1,0:T(8,128)(2,1)} async-done(((bf16[256,2048]{1,0:T(8,128)(2,1)}), bf16[2048,2048]{1,0:T(8,128)(2,1)}) %all-gather.6.cloned.1.call-update) | async-done | bytes 8388624 | tf_op jit(solution)/shard_map/all_gather | solution.py:12
  147.1 14.5 %multiply_reduce_fusion = (f32[1024]{0:T(1024)S(1)}, f32[1024,2048]{1,0:T(8,128)}) fusion(bf16[1024,2048]{1,0:T(8,128)(2,1)} %all-gather.4.cloned.1.call-done, bf16[2048,2048]{1,0:T(8,128)(2,1)} %all-gather.6.cloned.1.call-done), kind=kOutput, calls=%fused_computation | convolution fusion | flops 8594127872 | bytes 20975616 | tf_op jit(solution)/shard_map/dot_general | solution.py:8
  161.6 13.2 %all-gather = f32[4096]{0:T(1024)S(1)} all-gather(f32[1024]{0:T(1024)S(1)} %get-tuple-element.5), channel_id=2, replica_groups=mesh['gy'=8,'gx'=4] {'gx'}, dimensions={0}, use_global_device_ids=true | all-gather | bytes 20480 | tf_op jit(solution)/shard_map/all_gather | solution.py:16
  174.9 7.4 %broadcast_multiply_fusion = f32[1024,2048]{1,0:T(8,128)} fusion(f32[1024,2048]{1,0:T(8,128)} %get-tuple-element.6, f32[1024]{0:T(1024)S(1)} %add_rsqrt_fusion), kind=kLoop, calls=%fused_computation.1 | loop fusion | flops 2097152 | bytes 16781312 | tf_op jit(solution)/shard_map/mul | solution.py:19
  (3 shorter events, 0.0 us)
Async XLA Ops:
  6.5 85.9 %all-gather.4.cloned.1.call-start = ((), (), s32[]{:S(2)}) async-start(), calls=%async_computation | async-start | bytes 5242880 | tf_op jit(solution)/shard_map/all_gather | solution.py:13
  7.3 139.8 %all-gather.6.cloned.1.call-start = ((), (), s32[]{:S(2)}) async-start(), calls=%async_computation.1 | async-start | bytes 9437184 | tf_op jit(solution)/shard_map/all_gather | solution.py:12
Sparse Core Ops, SparseCore 0:
  8.9 83.4 all-gather.3
  94.3 52.7 all-gather.5
